TPU v7x, 32 devices: a whole 2x2x4 slice. The times are simulated.
32 devices in a mesh: dp: 4 (over z), mp: 8 (over y, x, core).
Axes of the slice: x: 2, y: 2, z: 4, core: 2. Of those that a mesh axis runs over, the one named last changes fastest.
Arguments:
- activations: bfloat16 [6144, 8192], P('dp', 'mp'), may hold values from -6 to 6
- grad_output: bfloat16 [6144, 16384], P('dp', 'mp'), may hold values from -0.078125 to 0.078125
- holder_index: int32 [8, 32, 1], replicated, may hold values from 0 to 7; in each aligned block of 32 rows (0 to 31, 32 to 63, ..., all dimensions but the last counted through in order) at most 4 rows name the same one
- row_offset: int32 [8, 32], replicated, may hold values from 0 to 7
- column_offset: int32 [8, 32], replicated, may hold values from 0 to 15
- live_counts: int32 [8], replicated, may hold values from 1 to 32, as said below
Outputs:
- candidate_grads: float32 [8, 32, 128, 128], P('mp', 'dp')
Inputs may be any that keep to these rules, and one draw needn't show every extreme that they name: In each owner's 32 slots at most 4 have the same holder_index, a bound that some block reaches. Slots from live_counts[o] on are unused; some owner uses all 32 slots.
All inputs are finite; a program needn't handle non-finite values.
Results may differ from a plain program's by a relative error of at most 0.0003.
Values may be sent and summed in bfloat16 or wider, within the bound.
No kernel may reach another device: no remote copies, remote signals or barrier semaphores. Data moves between devices by JAX's collectives and lax.ppermute only.
A program may use at most 192 MiB of HBM per device.

v0:
```python
import jax
import jax.numpy as jnp
from jax import lax
from jax.sharding import PartitionSpec as P

BLK = 128


def on_device(activations, grad_output, holder_index, row_offset, column_offset, live_counts):
    owners = lax.axis_size("mp")
    my_index = lax.axis_index("mp")
    tokens_here = activations.shape[0]
    block_size = BLK
    per_holder = activations.shape[1] // block_size
    per_owner = grad_output.shape[1] // block_size
    slot_count = row_offset.shape[1]
    holders_all = holder_index[:, :, 0]
    my_holder = lax.dynamic_index_in_dim(holders_all, my_index, 0, keepdims=False)
    my_offset = lax.dynamic_index_in_dim(row_offset, my_index, 0, keepdims=False)
    my_column = lax.dynamic_index_in_dim(column_offset, my_index, 0, keepdims=False)
    my_count = lax.dynamic_index_in_dim(live_counts, my_index, 0, keepdims=False)
    grad_panels = grad_output.reshape(tokens_here, per_owner, block_size)
    is_used = jnp.arange(slot_count, dtype=jnp.int32) < my_count
    gathered = lax.all_gather(activations, "mp", axis=1, tiled=True)
    input_panels = gathered.reshape(tokens_here, owners * per_holder, block_size)
    picked_input = jnp.take(input_panels, my_holder * per_holder + my_offset, axis=1)
    picked_grad = jnp.take(grad_panels, my_column, axis=1)
    blocks = jnp.einsum(
        "tkr,tkc->krc", picked_input, picked_grad, preferred_element_type=jnp.float32
    )
    blocks = jnp.where(is_used[:, None, None], blocks, jnp.zeros_like(blocks))
    summed = lax.psum_scatter(blocks, "dp", scatter_dimension=0, tiled=True)
    return summed[None]


def solution(mesh):
    placed = (P("dp", "mp"), P("dp", "mp"), P(), P(), P(), P())
    return jax.shard_map(
        on_device, mesh=mesh, in_specs=placed, out_specs=P("mp", "dp", None, None), check_vma=False
    )
```

profile of v0, /device:TPU:0, one launch (start us, length us, event | category | flops | bytes accessed | tf_op | source)
XLA Modules:
  0.0 249.4 jit_solution(7118658145184127169)
XLA Ops:
  6.5 0.0 all-gather.2.cloned.1.call-start
  6.5 4.6 %copy.9 = bf16[1536,1024]{0,1:T(8,128)(2,1)} copy(bf16[1536,1024]{1,0:T(8,128)(2,1)} %param.6) | data formatting | bytes 6291456 | tf_op args[0]
  11.2 0.0 all-gather.2.cloned.1.call-update
  11.2 0.0 reduce-scatter.2.cloned.1.call-start
  11.2 0.0 copy-start
  11.3 8.7 %copy.11 = bf16[1536,2048]{0,1:T(8,128)(2,1)} copy(bf16[1536,2048]{1,0:T(8,128)(2,1)} %param.7) | data formatting | bytes 12582912 | tf_op args[1]
  19.9 9.2 %copy.12 = bf16[1536,16,128]{2,0,1:T(8,128)(2,1)} copy(bf16[1536,16,128]{0,2,1:T(8,128)(2,1)} %bitcast.35) | data formatting | bytes 12582912 | tf_op jit(solution)/shard_map/reshape | solution.py:22
  29.1 0.0 copy-done
  29.1 0.6 dynamic_slice.14
  29.7 0.7 fusion.15
  30.4 9.4 %gather_fusion.1 = bf16[32,1536,128]{2,1,0:T(8,128)(2,1)} fusion(bf16[1536,16,128]{2,0,1:T(8,128)(2,1)} %copy.12, s32[1024]{0:T(1024)S(1)} %pad_clamp_fusion), kind=kCustom, calls=%fused_computation.1 | custom fusion | bytes 25165952 | tf_op jit(solution)/shard_map/jit(_take)/gather | solution.py:27
  39.9 0.6 iota_compare_fusion
  40.5 0.7 fusion.14
  41.2 0.7 compare_and_fusion
  41.9 97.3 %all-gather.2.cloned.1.call-done = bf16[1536,8192]{0,1:T(8,128)(2,1)} async-done(((bf16[1536,1024]{0,1:T(8,128)(2,1)}), bf16[1536,8192]{0,1:T(8,128)(2,1)}) %all-gather.2.cloned.1.call-update) | async-done | bytes 25165840 | tf_op jit(solution)/shard_map/all_gather | solution.py:24
  139.3 32.6 %copy.10 = bf16[1536,64,128]{2,0,1:T(8,128)(2,1)} copy(bf16[1536,64,128]{0,2,1:T(8,128)(2,1)} %bitcast.34) | data formatting | bytes 50331648 | tf_op jit(solution)/shard_map/reshape | solution.py:25
  171.8 14.9 %gather_fusion = bf16[32,1536,128]{2,1,0:T(8,128)(2,1)} fusion(bf16[1536,64,128]{2,0,1:T(8,128)(2,1)} %copy.10, s32[1024]{0:T(1024)S(1)} %pad_clamp_fusion.1), kind=kCustom, calls=%fused_computation | custom fusion | bytes 25165952 | tf_op jit(solution)/shard_map/jit(_take)/gather | solution.py:26
  186.8 12.0 %fusion.8 = f32[32,128,128]{2,1,0:T(8,128)} fusion(bf16[32,1536,128]{2,1,0:T(8,128)(2,1)} %gather_fusion.1, pred[32]{0:T(512)(128)(4,1)S(1)} %get-tuple-element.5, bf16[32,1536,128]{2,1,0:T(8,128)(2,1)} %gather_fusion, pred[32]{0:T(512)(128)(4,1)S(1)} %get-tuple-element.6, pred[32]{0:T(512)(128)(4,1)S(1)} %iota_compare_fusion), kind=kOutput, calls=%fused_computation.10 | convolution fusion | flops 1623719936 | bytes 27263072 | tf_op jit(solution)/shard_map/tkr,tkc->krc/dot_general | solution.py:28
  198.7 0.0 reduce-scatter.2.cloned.1.call-update
  198.7 43.8 %reduce-scatter.2.cloned.1.call-done = f32[8,128,128]{2,1,0:T(8,128)} async-done(((f32[32,128,128]{2,1,0:T(8,128)}), f32[8,128,128]{2,1,0:T(8,128)}) %reduce-scatter.2.cloned.1.call-update) | async-done | bytes 524304 | tf_op jit(solution)/shard_map/reduce_scatter | solution.py:32
  (2 shorter events, 0.0 us)
Async XLA Ops:
  6.5 132.7 %all-gather.2.cloned.1.call-start = ((), (), s32[]{:S(2)}) async-start(), calls=%async_computation.1 | async-start | bytes 28311552 | tf_op jit(solution)/shard_map/all_gather | solution.py:24
  11.2 231.3 %reduce-scatter.2.cloned.1.call-start = ((), (), s32[]{:S(2)}) async-start(), calls=%async_computation.2 | async-start | bytes 2621440 | tf_op jit(solution)/shard_map/reduce_scatter | solution.py:32
  11.2 17.9 %copy-start = (s32[8]{0:T(128)S(1)}, s32[8]{0:T(128)}, u32[]{:S(2)}) copy-start(s32[8]{0:T(128)} %param.11) | copy-start | bytes 100
Sparse Core Ops, SparseCore 0:
  11.3 127.9 all-gather.1
  198.9 43.6 reduce-scatter.1
where the time goes:
time: 251 us; the launch traced here: 249 us
  waiting for transfers between devices  141 us (56%)
  local copies, waits for them, and re-layouts  80 us (32%)
  between operations  13.4 us (5%)
  matrix products  12 us (5%)
  other arithmetic  2.77 us (1%)
    all_gather x1, waiting for transfers between devices, on_device(): gathered = lax.all_gather(activations, 'mp', axis=1, tiled=True)  97.3 us
    reduce_scatter x1, waiting for transfers between devices, on_device(): summed = lax.psum_scatter(blocks, 'dp', scatter_dimension=0, tiled=True)  43.8 us
    reshape x1, local copies, waits for them, and re-layouts, on_device(): gathered.reshape(tokens_here, owners * per_holder, block_size)  32.6 us
    gather x1, local copies, waits for them, and re-layouts, on_device(): jnp.take(input_panels, my_holder * per_holder + my_offset, axis=1)  14.9 us
    unnamed x4, local copies, waits for them, and re-layouts  13.3 us
    dot_general x1, matrix products, on_device(): jnp.einsum('tkr,tkc->krc', picked_input, picked_grad, preferred_element_t...  12 us
    gather x1, local copies, waits for them, and re-layouts, on_device(): picked_grad = jnp.take(grad_panels, my_column, axis=1)  9.45 us
    reshape x1, local copies, waits for them, and re-layouts, on_device(): grad_panels = grad_output.reshape(tokens_here, per_owner, block_size)  9.18 us
  transfers between devices with their start and end apart: 2, of which 2 were waited for; matrix products, arithmetic and copies ran while one was open for 12% of the time, Pallas kernels for 0%

commit v1 on v0

v1 whole, which is shorter than its diff:
```python
import functools

import jax
import jax.numpy as jnp
from jax import lax
from jax.experimental import pallas as pl
from jax.experimental.pallas import tpu as pltpu
from jax.sharding import PartitionSpec as P


BLK = 128


def gathered_plan(activations, grad_output, holder_index, row_offset, column_offset, live_counts):
    owners = lax.axis_size("mp")
    my_index = lax.axis_index("mp")
    tokens_here = activations.shape[0]
    per_holder = activations.shape[1] // BLK
    per_owner = grad_output.shape[1] // BLK
    slot_count = row_offset.shape[1]
    my_holder = lax.dynamic_index_in_dim(holder_index[:, :, 0], my_index, 0, keepdims=False)
    my_offset = lax.dynamic_index_in_dim(row_offset, my_index, 0, keepdims=False)
    my_column = lax.dynamic_index_in_dim(column_offset, my_index, 0, keepdims=False)
    my_count = lax.dynamic_index_in_dim(live_counts, my_index, 0, keepdims=False)
    grad_panels = grad_output.reshape(tokens_here, per_owner, BLK)
    is_used = jnp.arange(slot_count, dtype=jnp.int32) < my_count
    gathered = lax.all_gather(activations, "mp", axis=1, tiled=True)
    input_panels = gathered.reshape(tokens_here, owners * per_holder, BLK)
    picked_input = jnp.take(input_panels, my_holder * per_holder + my_offset, axis=1)
    picked_grad = jnp.take(grad_panels, my_column, axis=1)
    blocks = jnp.einsum(
        "tkr,tkc->krc", picked_input, picked_grad, preferred_element_type=jnp.float32
    )
    blocks = jnp.where(is_used[:, None, None], blocks, jnp.zeros_like(blocks))
    summed = lax.psum_scatter(blocks, "dp", scatter_dimension=0, tiled=True)
    return summed[None]


def chosen(values, places):
    ids = jnp.arange(values.shape[1], dtype=jnp.int32)
    return jnp.sum(jnp.where(places[:, :, None] == ids, values[:, None, :], 0), axis=2)


def two_colors(by_holder, by_share, steps):
    slots = by_holder.shape[1]
    jump = chosen(by_share, by_holder)
    least = jnp.broadcast_to(jnp.arange(slots, dtype=jnp.int32), jump.shape)
    for _ in range(steps):
        both = chosen(least + jump * slots, jump)
        least, jump = jnp.minimum(least, both % slots), both // slots
    return (least > chosen(least, by_holder)).astype(jnp.int32)


def slot_ranks(held, slots, per):
    ids = jnp.arange(slots, dtype=jnp.int32)
    same = held[:, :, None] == held[:, None, :]
    spot = jnp.sum((same & (ids[None, :] < ids[:, None])).astype(jnp.int32), axis=2)
    near = ids[None, :] // per == ids[:, None] // per
    by_holder = jnp.sum(jnp.where(same & (spot[:, None, :] == spot[:, :, None] ^ 1), ids, 0), axis=2)
    by_share = jnp.broadcast_to(ids ^ 1, held.shape)
    first = two_colors(by_holder, by_share, (slots // 2 - 1).bit_length())
    alike = (first[:, None, :] == first[:, :, None]) & (ids[None, :] != ids[:, None])
    by_holder = jnp.sum(jnp.where(same & alike, ids, 0), axis=2)
    by_share = jnp.sum(jnp.where(near & alike, ids, 0), axis=2)
    return 2 * first + two_colors(by_holder, by_share, (slots // 4 - 1).bit_length())


def slot_tables(holder_index, row_offset, column_offset, live_counts, owners, per_holder):
    slots = row_offset.shape[1]
    per = slots // owners
    held = holder_index[:, :, 0]
    ids = jnp.arange(slots, dtype=jnp.int32)
    owner = jnp.arange(owners, dtype=jnp.int32)[:, None]
    flip = owner ^ held
    rank = slot_ranks(held, slots, per)
    codes = jnp.arange(owners * per_holder, dtype=jnp.int32)
    same = (held * per_holder + row_offset)[:, :, None] == codes[None, None, :]
    panels = jnp.arange(per_holder, dtype=jnp.int32)
    by_x = (flip == 2) | (flip == 3) | (flip == 7)
    by_y = (flip == 4) | (flip == 5) | (flip == 6)

    def positions(by):
        value = jnp.where(by & (rank < 2), 2 - rank, 0)
        wanted = jnp.max(jnp.where(same, value[:, :, None], 0), axis=(0, 1))
        key = (2 - wanted.reshape(owners, per_holder)) * per_holder + panels[None, :]
        return jnp.sum((key[:, None, :] < key[:, :, None]).astype(jnp.int32), axis=2)

    x_spot, y_spot = positions(by_x), positions(by_y)
    spots = jnp.concatenate([x_spot, y_spot], axis=0)
    order = jnp.sum((spots[:, None, :] == panels[None, :, None]).astype(jnp.int32) * panels, axis=2)
    spot = jnp.where(
        by_x[:, :, None], x_spot.reshape(-1)[None, None, :], y_spot.reshape(-1)[None, None, :]
    )
    spot = jnp.sum(jnp.where(same, spot, 0), axis=2)
    used = (ids[None, :] < live_counts[:, None]).astype(jnp.int32)
    packed = row_offset + (column_offset << 8) + (used << 16) + (spot << 17)
    hit = (held * per + rank)[:, None, :] == ids[None, :, None]
    words = jnp.sum(jnp.where(hit, packed[:, None, :], 0), axis=2)
    fills = (rank * (slots // per) + ids // per)[:, None, :] == ids[None, :, None]
    fillers = jnp.sum(jnp.where(fills, (flip + owners * (ids % per))[:, None, :], 0), axis=2)
    return words, order, fillers


def row_of(word):
    return word & 255


def column_of(word):
    return (word >> 8) & 255


def used_of(word):
    return (word >> 16) & 1


def spot_of(word):
    return word >> 17


ANY = pl.BlockSpec(memory_space=pl.ANY)
SMEM = pl.BlockSpec(memory_space=pltpu.SMEM)
VMEM = pl.BlockSpec(memory_space=pltpu.VMEM)
COST = 4 * 1536 * BLK * BLK


def work(count):
    return pl.CostEstimate(flops=int(count * COST), bytes_accessed=0, transcendentals=0)


def panel_copies(head, pieces, word, to, sems):
    spot = spot_of(word)
    column = pl.multiple_of(row_of(word) * BLK, BLK)
    cut = head.shape[0]
    rest = to.shape[0] - cut
    first = pltpu.make_async_copy(head.at[:, pl.ds(column, BLK)], to.at[pl.ds(0, cut)], sems.at[0])
    first.start()
    low = 0
    for piece in pieces:
        size = piece.shape[0]
        place = jnp.clip(spot - low, 0, size - 1)
        copy = pltpu.make_async_copy(piece.at[place], to.at[pl.ds(cut, rest)], sems.at[1])
        if len(pieces) == 1:
            copy.start()
        else:
            pl.when((spot >= low) & (spot < low + size))(copy.start)
        low += size
    return [first, pltpu.make_async_copy(pieces[0].at[0], to.at[pl.ds(cut, rest)], sems.at[1])]


def send_panels(me, order, shard, cut, low, high, owners, after=()):
    rest = shard.shape[0] - cut
    count = high - low

    def body(me_ref, order_ref, shard_ref, *refs):
        x_ref, y_ref, held, arrived, left = refs[-5:]
        moves = []
        for way, ref in enumerate((x_ref, y_ref)):
            for k in range(count):
                n = way * count + k
                start = pl.multiple_of(order_ref[me_ref[0] + way * owners, low + k] * BLK, BLK)
                source = shard_ref.at[pl.ds(cut, rest), pl.ds(start, BLK)]
                moves.append(
                    (
                        pltpu.make_async_copy(source, held.at[n], arrived.at[n]),
                        pltpu.make_async_copy(held.at[n], ref.at[k], left.at[n]),
                    )
                )
        for come, _ in moves:
            come.start()
        for come, go in moves:
            come.wait()
            go.start()
        for _, go in moves:
            go.wait()

    return pl.pallas_call(
        body,
        in_specs=[SMEM, SMEM, ANY] + [ANY] * len(after),
        out_specs=[ANY, ANY],
        out_shape=[jax.ShapeDtypeStruct((count, rest, BLK), shard.dtype)] * 2,
        scratch_shapes=[
            pltpu.VMEM((2 * count, rest, BLK), shard.dtype),
            pltpu.SemaphoreType.DMA((2 * count,)),
            pltpu.SemaphoreType.DMA((2 * count,)),
        ],
        cost_estimate=work(count),
        name="send_panels",
    )(me, order, shard, *after)


def pass_panels(me, words, x_source, y_source, ranks, per, tokens, after):
    flat = [*x_source, *y_source]
    parts = len(x_source)
    total = 2 * len(ranks)

    def body(me_ref, words_ref, *refs):
        ins, (held, arrived, left) = refs[: 2 * parts], refs[-3:]
        outs = refs[-3 - total : -3]
        me = me_ref[0]
        moves = []
        for n in range(total):
            source, owner_flip, holder_flip = ((ins[parts:], 2, 4), (ins[:parts], 5, 2))[n % 2]
            word = words_ref[me ^ owner_flip, (me ^ holder_flip) * per + ranks[n // 2]]
            come = panel_copies(source[0], source[1:], word, held.at[n], arrived.at[n])
            moves.append((come, pltpu.make_async_copy(held.at[n], outs[n].at[0], left.at[n])))
        for come, go in moves:
            for copy in come:
                copy.wait()
            go.start()
        for _, go in moves:
            go.wait()

    return pl.pallas_call(
        body,
        in_specs=[SMEM, SMEM] + [ANY] * (len(flat) + len(after)),
        out_specs=[ANY] * total,
        out_shape=[jax.ShapeDtypeStruct((1, tokens, BLK), flat[0].dtype)] * total,
        scratch_shapes=[
            pltpu.VMEM((total, tokens, BLK), flat[0].dtype),
            pltpu.SemaphoreType.DMA((total, 2)),
            pltpu.SemaphoreType.DMA((total,)),
        ],
        cost_estimate=work(total / 2),
        name="pass_panels",
    )(me, words, *flat, *after)


def product(panel, grad):
    return lax.dot_general(panel, grad, (((0,), (0,)), ((), ())), preferred_element_type=jnp.float32)


def grad_copy(grad_ref, word, to, sem):
    column = pl.multiple_of(column_of(word) * BLK, BLK)
    copy = pltpu.make_async_copy(grad_ref.at[:, pl.ds(column, BLK)], to, sem)
    copy.start()
    return copy


def block_grads(me, words, grad, sources, flips, ranks, per, after=()):
    count = len(ranks)
    tokens = grad.shape[0]
    total = len(flips) * count
    arrays = [array for source in sources for array in source]

    def body(me_ref, words_ref, *refs):
        out_ref, inputs, grads, input_sems, grad_sems = refs[-5:]
        grad_ref = refs[len(arrays)]
        me = me_ref[0]
        waits, lives = [], []
        at = 0
        for k, source in enumerate(sources):
            own = refs[at : at + len(source)]
            at += len(own)
            for r, rank in enumerate(ranks):
                n = k * count + r
                word = words_ref[me, (me ^ flips[k]) * per + rank]
                lives.append(used_of(word) > 0)
                copies = [grad_copy(grad_ref, word, grads.at[n], grad_sems.at[n])]
                if len(own) == 1:
                    row = pl.multiple_of(row_of(word) * BLK, BLK)
                    copy = pltpu.make_async_copy(
                        own[0].at[:, pl.ds(row, BLK)], inputs.at[n], input_sems.at[n, 0]
                    )
                    copy.start()
                    copies.append(copy)
                else:
                    copies += panel_copies(own[0], own[1:], word, inputs.at[n], input_sems.at[n])
                waits.append(copies)
        for n in range(total):
            for copy in waits[n]:
                copy.wait()
            block = product(inputs[n], grads[n])
            out_ref[n] = jnp.where(lives[n], block, jnp.zeros_like(block))

    return pl.pallas_call(
        body,
        in_specs=[SMEM, SMEM] + [ANY] * (len(arrays) + 1 + len(after)),
        out_specs=VMEM,
        out_shape=jax.ShapeDtypeStruct((total, BLK, BLK), jnp.float32),
        scratch_shapes=[
            pltpu.VMEM((total, tokens, BLK), grad.dtype),
            pltpu.VMEM((total, tokens, BLK), grad.dtype),
            pltpu.SemaphoreType.DMA((total, 2)),
            pltpu.SemaphoreType.DMA((total,)),
        ],
        cost_estimate=work(total),
        name="block_grads",
    )(me, words, *arrays, grad, *after)


def finish_rank(meta, words, fillers, grad, far, zero, near, near_step, near_at, rank, per, groups, owners, after=()):
    tokens = grad.shape[0]
    share = owners // groups

    def body(meta_ref, words_ref, fillers_ref, *refs):
        far_refs, grad_ref, zero_ref, near_ref = refs[:2], refs[2], refs[3], refs[4]
        outs = refs[-5 - groups : -5]
        inputs, grads, blocks, input_sems, grad_sems = refs[-5:]
        me, group = meta_ref[0], meta_ref[1]
        waits, lives = [], []
        for n in range(2):
            word = words_ref[me, (me ^ (6 + n)) * per + rank]
            lives.append(used_of(word) > 0)
            copy = pltpu.make_async_copy(far_refs[n].at[0], inputs.at[n], input_sems.at[n])
            copy.start()
            waits.append([copy, grad_copy(grad_ref, word, grads.at[n], grad_sems.at[n])])
        blocks[0] = zero_ref[rank]
        blocks[1] = zero_ref[per + rank]
        for n, flip in enumerate((2, 4, 3, 5)):
            blocks[flip] = near_ref[n * near_step + near_at]
        for n in range(2):
            for copy in waits[n]:
                copy.wait()
            block = product(inputs[n], grads[n])
            blocks[6 + n] = jnp.where(lives[n], block, jnp.zeros_like(block))
        for step, out in enumerate(outs):
            to = lax.rem(group + step, groups)
            for k in range(share):
                flip = lax.rem(fillers_ref[me, rank * owners + to * share + k], owners)
                out[k] = blocks[flip]

    return pl.pallas_call(
        body,
        in_specs=[SMEM, SMEM, SMEM, ANY, ANY, ANY, VMEM, VMEM] + [ANY] * len(after),
        out_specs=[VMEM] * groups,
        out_shape=[jax.ShapeDtypeStruct((share, BLK, BLK), jnp.float32)] * groups,
        scratch_shapes=[
            pltpu.VMEM((2, tokens, BLK), grad.dtype),
            pltpu.VMEM((2, tokens, BLK), grad.dtype),
            pltpu.VMEM((owners, BLK, BLK), jnp.float32),
            pltpu.SemaphoreType.DMA((2,)),
            pltpu.SemaphoreType.DMA((2,)),
        ],
        cost_estimate=work(2),
        name="finish_rank",
    )(meta, words, fillers, *far, grad, zero, near, *after)


def place_sums(meta, fillers, ranks, owners, per):
    groups = len(ranks[0])
    share = owners // groups

    def body(meta_ref, fillers_ref, *refs):
        out_ref = refs[-1]
        for r in range(len(ranks)):
            parts = refs[r * groups : (r + 1) * groups]
            for k in range(share):
                filler = fillers_ref[meta_ref[0], r * owners + meta_ref[1] * share + k]
                block = parts[0][k]
                for part in parts[1:]:
                    block = block + part[k]
                out_ref[k * per + filler // owners] = block

    flat = [part for parts in ranks for part in parts]
    return pl.pallas_call(
        body,
        in_specs=[SMEM, SMEM] + [VMEM] * len(flat),
        out_specs=VMEM,
        out_shape=jax.ShapeDtypeStruct((share * per, BLK, BLK), jnp.float32),
        cost_estimate=work(1),
        name="place_sums",
    )(meta, fillers, *flat)


def flipped(array, bits):
    count = lax.axis_size("mp")
    return lax.ppermute(array, "mp", [(i, i ^ bits) for i in range(count)])


def turned(array, step):
    count = lax.axis_size("dp")
    return lax.ppermute(array, "dp", [(i, (i + step) % count) for i in range(count)])


def square_plan(activations, grad_output, holder_index, row_offset, column_offset, live_counts):
    owners = lax.axis_size("mp")
    groups = lax.axis_size("dp")
    index = lax.axis_index("mp").astype(jnp.int32)
    group = lax.axis_index("dp").astype(jnp.int32)
    slots = row_offset.shape[1]
    per = slots // owners
    tokens = activations.shape[0]
    per_holder = activations.shape[1] // BLK
    cut = tokens // 3 // 16 * 16
    me = index.reshape(1)

    head = activations[:cut]
    x_head, y_head = flipped(head, 2), flipped(head, 4)
    twin = flipped(activations, 1)
    words, order, fillers = slot_tables(
        holder_index, row_offset, column_offset, live_counts, owners, per_holder
    )
    meta = jnp.stack([index, group])
    send = functools.partial(send_panels, me, order, activations, cut, owners=owners)
    grads = functools.partial(block_grads, me, words, grad_output, per=per)
    pass_on = functools.partial(pass_panels, me, words, per=per, tokens=tokens)
    finish = functools.partial(
        finish_rank, meta, words, fillers, grad_output, per=per, groups=groups, owners=owners
    )

    def finished(rank, near, near_step, near_at, after=()):
        parts = finish(far[rank], zero, near, near_step, near_at, rank, after=after)
        return parts, [parts[0]] + [turned(parts[step], step) for step in range(1, groups)]

    go = send(0, 3)
    x_0, y_0 = flipped(go[0], 2), flipped(go[1], 4)
    go = send(3, 6, after=go)
    x_1, y_1 = flipped(go[0], 2), flipped(go[1], 4)
    xt_head, yt_head = flipped(x_head, 1), flipped(y_head, 1)
    zero = grads([(activations,), (twin,)], [0, 1], list(range(per)), after=(*go, fillers, meta))

    far = []
    xt_0, yt_0 = flipped(x_0, 1), flipped(y_0, 1)
    go = pass_on((x_head, x_0), (y_head, y_0), [0], after=(zero,))
    far.append((flipped(go[0], 2), flipped(go[1], 5)))
    go = send(6, per_holder, after=go)
    x_2, y_2 = flipped(go[0], 2), flipped(go[1], 4)
    flips = [2, 4, 3, 5]
    near_0 = grads(
        [(x_head, x_0), (y_head, y_0), (xt_head, xt_0), (yt_head, yt_0)], flips, [0], after=go
    )
    xt_1, yt_1 = flipped(x_1, 1), flipped(y_1, 1)
    go = pass_on((x_head, x_0, x_1), (y_head, y_0, y_1), [1], after=(near_0,))
    far.append((flipped(go[0], 2), flipped(go[1], 5)))
    near_1 = grads(
        [(x_head, x_0, x_1), (y_head, y_0, y_1), (xt_head, xt_0, xt_1), (yt_head, yt_0, yt_1)],
        flips, [1], after=go,
    )
    parts, sum_0 = finished(0, near_0, 1, 0, after=(near_1,))
    xt_2, yt_2 = flipped(x_2, 1), flipped(y_2, 1)
    late = list(range(2, per))
    go = pass_on((x_head, x_0, x_1, x_2), (y_head, y_0, y_1, y_2), late, after=(parts[0],))
    for n, rank in enumerate(late):
        far.append((flipped(go[2 * n], 2), flipped(go[2 * n + 1], 5)))
    near_2 = grads(
        [(x_head, x_0, x_1, x_2), (y_head, y_0, y_1, y_2), (xt_head, xt_0, xt_1, xt_2), (yt_head, yt_0, yt_1, yt_2)],
        flips, late, after=go,
    )
    parts, sum_1 = finished(1, near_1, 1, 0, after=(near_2,))
    sums = [sum_0, sum_1]
    for n, rank in enumerate(late):
        parts, sum_n = finished(rank, near_2, len(late), n, after=(parts[0],))
        sums.append(sum_n)
    out = place_sums(meta, fillers, sums, owners, per)
    return out[None]


def solution(mesh):
    placed = (P("dp", "mp"), P("dp", "mp"), P(), P(), P(), P())
    square = (mesh.shape["mp"], mesh.shape["dp"]) == (8, 4)

    def body(*arrays):
        return (square_plan if square else gathered_plan)(*arrays)

    return jax.shard_map(
        body, mesh=mesh, in_specs=placed, out_specs=P("mp", "dp", None, None), check_vma=False
    )
```

time: 251 us -> 196 us (0.78)
  local copies, waits for them, and re-layouts: 80 us -> 6.42 us
  waiting for transfers between devices: 141 us -> 76.3 us
  Pallas kernels: 0 us -> 55.2 us
  starting transfers between devices: 0.04 us -> 43.8 us
  between operations: 13.4 us -> 0.69 us
  matrix products: 12 us -> 0 us
  other arithmetic: 2.77 us -> 12.4 us
    all_gather x1 -> x0, waiting for transfers between devices: 97.3 us -> none  [on_device(): gathered = lax.all_gather(activations, 'mp', axis=1, tiled=True)]
    ppermute x0 -> x37, waiting for transfers between devices: none -> 76.3 us  [the longest x25 64.6 us: flipped(): return lax.ppermute(array, 'mp', [(i, i ^ bits) for i in range(count)])]
    pallas_call x0 -> x15, Pallas kernels: none -> 55.2 us  [the longest x4 19.6 us: block_grads(): pl.pallas_call(body, in_specs=[SMEM, SMEM] + [ANY] * (len(arrays) + 1 + l...]
    reduce_scatter x1 -> x0, waiting for transfers between devices: 43.8 us -> none  [on_device(): summed = lax.psum_scatter(blocks, 'dp', scatter_dimension=0, tiled=True)]
    ppermute x0 -> x37, starting transfers between devices: none -> 43.8 us  [the longest x12 26 us: turned(): lax.ppermute(array, 'dp', [(i, (i + step) % count) for i in range(count)])]
    reshape x2 -> x0, local copies, waits for them, and re-layouts: 41.8 us -> none  [the longest x1 32.6 us: on_device(): gathered.reshape(tokens_here, owners * per_holder, block_size)]
    gather x2 -> x0, local copies, waits for them, and re-layouts: 24.4 us -> none  [the longest x1 14.9 us: on_device(): jnp.take(input_panels, my_holder * per_holder + my_offset, axis=1)]
    dot_general x1 -> x0, matrix products: 12 us -> none  [on_device(): jnp.einsum('tkr,tkc->krc', picked_input, picked_grad, preferred_element_t...]
  transfers between devices with their start and end apart: 2 -> 37, of which waited for: 2 -> 11; matrix products, arithmetic and copies ran while one was open for 12% -> 8% of each run, Pallas kernels for 0% -> 27%
where the time goes in v1:
time: 196 us; the launch traced here: 195 us
  waiting for transfers between devices  76.3 us (39%)
  Pallas kernels  55.2 us (28%)
  starting transfers between devices  43.8 us (22%)
  other arithmetic  12.4 us (6%)
  local copies, waits for them, and re-layouts  6.42 us (3%)
    ppermute x25, waiting for transfers between devices, flipped(): return lax.ppermute(array, 'mp', [(i, i ^ bits) for i in range(count)])  64.6 us
    ppermute x12, starting transfers between devices, turned(): lax.ppermute(array, 'dp', [(i, (i + step) % count) for i in range(count)])  26 us
    pallas_call x4, Pallas kernels, block_grads(): pl.pallas_call(body, in_specs=[SMEM, SMEM] + [ANY] * (len(arrays) + 1 + l...  19.6 us
    ppermute x25, starting transfers between devices, flipped(): return lax.ppermute(array, 'mp', [(i, i ^ bits) for i in range(count)])  17.8 us
    pallas_call x4, Pallas kernels, finish_rank(): pl.pallas_call(body, in_specs=[SMEM, SMEM, SMEM, ANY, ANY, ANY, VMEM, VME...  15.6 us
    ppermute x12, waiting for transfers between devices, turned(): lax.ppermute(array, 'dp', [(i, (i + step) % count) for i in range(count)])  11.7 us
    pallas_call x3, Pallas kernels, send_panels(): pl.pallas_call(body, in_specs=[SMEM, SMEM, ANY] + [ANY] * len(after), out...  8.99 us
    pallas_call x3, Pallas kernels, pass_panels(): pl.pallas_call(body, in_specs=[SMEM, SMEM] + [ANY] * (len(flat) + len(aft...  8.53 us
  transfers between devices with their start and end apart: 37, of which 11 were waited for; matrix products, arithmetic and copies ran while one was open for 8% of the time, Pallas kernels for 27%

profile of v1, /device:TPU:0, one launch (start us, length us, event | category | flops | bytes accessed | tf_op | source)
XLA Modules:
  0.0 194.8 jit_solution(5096625425110400405)
XLA Ops:
  11.3 3.0 %send_panels.3 = (bf16[3,1024,128]{2,1,0:T(8,128)(2,1)}, bf16[3,1024,128]{2,1,0:T(8,128)(2,1)}) custom-call(s32[1]{0:T(128)} %bitcast.me_ref, s32[16,8]{1,0:T(8,128)} %copy.10.order_ref, bf16[1536,1024]{1,0:T(8,128)(2,1)} %shard_ref.5), custom_call_target="tpu_custom_call" | custom-call | flops 301989888 | tf_op jit(solution)/shard_map/send_panels/pallas_call | solution.py:176
  14.3 2.6 %collective-permute-start.1 = (bf16[3,1024,128]{2,1,0:T(8,128)(2,1)}, bf16[3,1024,128]{2,1,0:T(8,128)(2,1)S(1)}, u32[]{:S(2)}, u32[]{:S(2)}) collective-permute-start(bf16[3,1024,128]{2,1,0:T(8,128)(2,1)} %get-tuple-element.35.refs_0_), channel_id=1, source_target_pairs={{0,2},{1,3},{2,0},{3,1},{4,6},{5,7},{6,4},{7,5},{8,10},{9,11},{10,... | collective-permute-start | bytes 2359304 | tf_op jit(solution)/shard_map/ppermute | solution.py:367
  18.4 3.0 %send_panels.4 = (bf16[3,1024,128]{2,1,0:T(8,128)(2,1)}, bf16[3,1024,128]{2,1,0:T(8,128)(2,1)}) custom-call(s32[1]{0:T(128)} %bitcast.me_ref, s32[16,8]{1,0:T(8,128)} %copy.10.order_ref, bf16[1536,1024]{1,0:T(8,128)(2,1)} %shard_ref.5, bf16[3,1024,128]{2,1,0:T(8,128)(2,1)} %get-tuple-element.35.refs_0_, bf16[3,1024,128]{2,1,0:T(8,128)(2,1)} %get-tuple-element.36.refs_1_), custom_call_target="tpu_custom_call" | custom-call | flops 301989888 | tf_op jit(solution)/shard_map/send_panels/pallas_call | solution.py:176
  22.0 2.3 %slice.3 = bf16[512,1024]{1,0:T(8,128)(2,1)} slice(bf16[1536,1024]{1,0:T(8,128)(2,1)} %shard_ref.5), slice={[0:512], [0:1024]} | slice | bytes 2097152 | tf_op jit(solution)/shard_map/slice | solution.py:387
  24.4 11.1 %collective-permute-done.1.refs_1_ = bf16[3,1024,128]{2,1,0:T(8,128)(2,1)S(1)} collective-permute-done((bf16[3,1024,128]{2,1,0:T(8,128)(2,1)}, bf16[3,1024,128]{2,1,0:T(8,128)(2,1)S(1)}, u32[]{:S(2)}, u32[]{:S(2)}) %collective-permute-start.1) | collective-permute-done | bytes 786464 | tf_op jit(solution)/shard_map/ppermute | solution.py:367
  35.5 2.0 %collective-permute-start = (bf16[512,1024]{1,0:T(8,128)(2,1)}, bf16[512,1024]{1,0:T(8,128)(2,1)S(1)}, u32[]{:S(2)}, u32[]{:S(2)}) collective-permute-start(bf16[512,1024]{1,0:T(8,128)(2,1)} %slice.3), channel_id=1, source_target_pairs={{0,2},{1,3},{2,0},{3,1},{4,6},{5,7},{6,4},{7,5},{8,10},{9,11},{10,... | collective-permute-start | bytes 3145736 | tf_op jit(solution)/shard_map/ppermute | solution.py:367
  39.2 13.3 %collective-permute-done.11.refs_2_ = bf16[3,1024,128]{2,1,0:T(8,128)(2,1)} collective-permute-done((bf16[3,1024,128]{2,1,0:T(8,128)(2,1)}, bf16[3,1024,128]{2,1,0:T(8,128)(2,1)}, u32[]{:S(2)}, u32[]{:S(2)}) %collective-permute-start.11) | collective-permute-done | bytes 786464 | tf_op jit(solution)/shard_map/ppermute | solution.py:367
  52.6 7.4 %collective-permute-done.2.refs_2_.refs_3_.refs_4_ = bf16[512,1024]{1,0:T(8,128)(2,1)S(1)} collective-permute-done((bf16[512,1024]{1,0:T(8,128)(2,1)}, bf16[512,1024]{1,0:T(8,128)(2,1)S(1)}, u32[]{:S(2)}, u32[]{:S(2)}) %collective-permute-start.2) | collective-permute-done | bytes 1048608 | tf_op jit(solution)/shard_map/ppermute | solution.py:367
  60.0 14.6 %collective-permute-done.refs_0_ = bf16[512,1024]{1,0:T(8,128)(2,1)S(1)} collective-permute-done((bf16[512,1024]{1,0:T(8,128)(2,1)}, bf16[512,1024]{1,0:T(8,128)(2,1)S(1)}, u32[]{:S(2)}, u32[]{:S(2)}) %collective-permute-start) | collective-permute-done | bytes 1048608 | tf_op jit(solution)/shard_map/ppermute | solution.py:367
  79.4 5.3 %block_grads.4.refs_4_.refs_3_ = f32[8,128,128]{2,1,0:T(8,128)} custom-call(s32[1]{0:T(128)} %bitcast.me_ref, s32[8,32]{1,0:T(8,128)} %select_reduce_fusion.words_ref, bf16[1536,1024]{1,0:T(8,128)(2,1)} %shard_ref.5, bf16[1536,1024]{1,0:T(8,128)(2,1)} %collective-permute-done.4.refs_1_, bf16[1536,2048]{1,0:T(8,128)(2,1)} %refs_2_.9, ...), custom_call_target="tpu_custom_call" | custom-call | flops 805306368 | tf_op jit(solution)/shard_map/block_grads/pallas_call | solution.py:275
  84.8 2.7 %pass_panels.3 = (bf16[1,1536,128]{2,1,0:T(8,128)(2,1)}, bf16[1,1536,128]{2,1,0:T(8,128)(2,1)}) custom-call(s32[1]{0:T(128)} %bitcast.me_ref, s32[8,32]{1,0:T(8,128)} %select_reduce_fusion.words_ref, bf16[512,1024]{1,0:T(8,128)(2,1)} %copy-done.1, bf16[3,1024,128]{2,1,0:T(8,128)(2,1)} %copy-done.2, bf16[512,1024]{1,0:T(8,128)(2,1)} %copy-done, ...), custom_call_target="tpu_custom_call" | custom-call | flops 100663296 | tf_op jit(solution)/shard_map/pass_panels/pallas_call | solution.py:213
  87.5 3.0 %send_panels.5 = (bf16[2,1024,128]{2,1,0:T(8,128)(2,1)}, bf16[2,1024,128]{2,1,0:T(8,128)(2,1)}) custom-call(s32[1]{0:T(128)} %bitcast.me_ref, s32[16,8]{1,0:T(8,128)} %copy.10.order_ref, bf16[1536,1024]{1,0:T(8,128)(2,1)} %shard_ref.5, bf16[1,1536,128]{2,1,0:T(8,128)(2,1)} %get-tuple-element.39.refs_0_, bf16[1,1536,128]{2,1,0:T(8,128)(2,1)} %get-tuple-element.40.refs_1_), custom_call_target="tpu_custom_call" | custom-call | flops 201326592 | tf_op jit(solution)/shard_map/send_panels/pallas_call | solution.py:176
  94.1 4.1 %block_grads.5.refs_6_.refs_4_ = f32[4,128,128]{2,1,0:T(8,128)} custom-call(s32[1]{0:T(128)} %bitcast.me_ref, s32[8,32]{1,0:T(8,128)} %select_reduce_fusion.words_ref, bf16[512,1024]{1,0:T(8,128)(2,1)} %copy-done.1, bf16[3,1024,128]{2,1,0:T(8,128)(2,1)} %copy-done.2, bf16[512,1024]{1,0:T(8,128)(2,1)} %copy-done, ...), custom_call_target="tpu_custom_call" | custom-call | flops 402653184 | tf_op jit(solution)/shard_map/block_grads/pallas_call | solution.py:275
  98.2 2.7 %pass_panels.4 = (bf16[1,1536,128]{2,1,0:T(8,128)(2,1)}, bf16[1,1536,128]{2,1,0:T(8,128)(2,1)}) custom-call(s32[1]{0:T(128)} %bitcast.me_ref, s32[8,32]{1,0:T(8,128)} %select_reduce_fusion.words_ref, bf16[512,1024]{1,0:T(8,128)(2,1)} %copy-done.1, bf16[3,1024,128]{2,1,0:T(8,128)(2,1)} %copy-done.2, bf16[3,1024,128]{2,1,0:T(8,128)(2,1)} %collective-permute-done.11.refs_2_, ...), custom_call_target="tpu_custom_call" | custom-call | flops 100663296 | tf_op jit(solution)/shard_map/pass_panels/pallas_call | solution.py:213
  101.8 4.2 %block_grads.6.refs_5_.refs_4_ = f32[4,128,128]{2,1,0:T(8,128)} custom-call(s32[1]{0:T(128)} %bitcast.me_ref, s32[8,32]{1,0:T(8,128)} %select_reduce_fusion.words_ref, bf16[512,1024]{1,0:T(8,128)(2,1)} %copy-done.1, bf16[3,1024,128]{2,1,0:T(8,128)(2,1)} %copy-done.2, bf16[3,1024,128]{2,1,0:T(8,128)(2,1)} %collective-permute-done.11.refs_2_, ...), custom_call_target="tpu_custom_call" | custom-call | flops 402653184 | tf_op jit(solution)/shard_map/block_grads/pallas_call | solution.py:275
  106.0 8.0 %collective-permute-done.5.refs_0_ = bf16[1,1536,128]{2,1,0:T(8,128)(2,1)S(1)} collective-permute-done((bf16[1,1536,128]{2,1,0:T(8,128)(2,1)S(1)}, bf16[1,1536,128]{2,1,0:T(8,128)(2,1)S(1)}, u32[]{:S(2)}, u32[]{:S(2)}) %collective-permute-start.5) | collective-permute-done | bytes 393248 | tf_op jit(solution)/shard_map/ppermute | solution.py:367
  115.5 3.8 %finish_rank.4 = (f32[2,128,128]{2,1,0:T(8,128)}, f32[2,128,128]{2,1,0:T(8,128)}, f32[2,128,128]{2,1,0:T(8,128)}, f32[2,128,128]{2,1,0:T(8,128)}) custom-call(s32[2]{0:T(128)} %pad_add_fusion.1.refs_6_.meta_ref, s32[8,32]{1,0:T(8,128)} %select_reduce_fusion.words_ref, s32[8,32]{1,0:T(8,128)} %select_reduce_fusion.4.refs_5_.fillers_ref, ...), custom_call_target="tpu_custom_call" | custom-call | flops 201326592 | tf_op jit(solution)/shard_map/finish_rank/pallas_call | solution.py:322
  120.4 3.1 %pass_panels.5 = (bf16[1,1536,128]{2,1,0:T(8,128)(2,1)}, bf16[1,1536,128]{2,1,0:T(8,128)(2,1)}, bf16[1,1536,128]{2,1,0:T(8,128)(2,1)}, bf16[1,1536,128]{2,1,0:T(8,128)(2,1)}) custom-call(s32[1]{0:T(128)} %bitcast.me_ref, s32[8,32]{1,0:T(8,128)} %select_reduce_fusion.words_ref, bf16[512,1024]{1,0:T(8,128)(2,1)} %copy-done.1, bf16[3,1024,128]{2,1,0:T(8,128)(2,1)} %copy-done.2, ...), custom_call_target="tpu_custom_call" | custom-call | flops 201326592 | tf_op jit(solution)/shard_map/pass_panels/pallas_call | solution.py:213
  127.2 8.5 %collective-permute-done.27.refs_0_ = bf16[1,1536,128]{2,1,0:T(8,128)(2,1)S(1)} collective-permute-done((bf16[1,1536,128]{2,1,0:T(8,128)(2,1)}, bf16[1,1536,128]{2,1,0:T(8,128)(2,1)S(1)}, u32[]{:S(2)}, u32[]{:S(2)}) %collective-permute-start.27) | collective-permute-done | bytes 393248 | tf_op jit(solution)/shard_map/ppermute | solution.py:367
  137.6 2.6 %collective-permute-start.16 = (f32[2,128,128]{2,1,0:T(8,128)}, f32[2,128,128]{2,1,0:T(8,128)}, u32[]{:S(2)}, u32[]{:S(2)}) collective-permute-start(f32[2,128,128]{2,1,0:T(8,128)} %get-tuple-element.47), channel_id=1, source_target_pairs={{0,16},{8,24},{16,0},{24,8},{1,17},{9,25},{17,1},{25,9},{2,18},{10... | collective-permute-start | bytes 393224 | tf_op jit(solution)/shard_map/ppermute | solution.py:372
  140.1 6.0 %block_grads.7.refs_5_.refs_4_ = f32[8,128,128]{2,1,0:T(8,128)} custom-call(s32[1]{0:T(128)} %bitcast.me_ref, s32[8,32]{1,0:T(8,128)} %select_reduce_fusion.words_ref, bf16[512,1024]{1,0:T(8,128)(2,1)} %copy-done.1, bf16[3,1024,128]{2,1,0:T(8,128)(2,1)} %copy-done.2, bf16[3,1024,128]{2,1,0:T(8,128)(2,1)} %collective-permute-done.11.refs_2_, ...), custom_call_target="tpu_custom_call" | custom-call | flops 805306368 | tf_op jit(solution)/shard_map/block_grads/pallas_call | solution.py:275
  146.2 3.9 %finish_rank.5 = (f32[2,128,128]{2,1,0:T(8,128)}, f32[2,128,128]{2,1,0:T(8,128)}, f32[2,128,128]{2,1,0:T(8,128)}, f32[2,128,128]{2,1,0:T(8,128)}) custom-call(s32[2]{0:T(128)} %pad_add_fusion.1.refs_6_.meta_ref, s32[8,32]{1,0:T(8,128)} %select_reduce_fusion.words_ref, s32[8,32]{1,0:T(8,128)} %select_reduce_fusion.4.refs_5_.fillers_ref, ...), custom_call_target="tpu_custom_call" | custom-call | flops 201326592 | tf_op jit(solution)/shard_map/finish_rank/pallas_call | solution.py:322
  151.6 4.0 %finish_rank.6 = (f32[2,128,128]{2,1,0:T(8,128)}, f32[2,128,128]{2,1,0:T(8,128)}, f32[2,128,128]{2,1,0:T(8,128)}, f32[2,128,128]{2,1,0:T(8,128)}) custom-call(s32[2]{0:T(128)} %pad_add_fusion.1.refs_6_.meta_ref, s32[8,32]{1,0:T(8,128)} %select_reduce_fusion.words_ref, s32[8,32]{1,0:T(8,128)} %select_reduce_fusion.4.refs_5_.fillers_ref, ...), custom_call_target="tpu_custom_call" | custom-call | flops 201326592 | tf_op jit(solution)/shard_map/finish_rank/pallas_call | solution.py:322
  157.1 2.4 %collective-permute-start.26 = (f32[2,128,128]{2,1,0:T(8,128)S(1)}, f32[2,128,128]{2,1,0:T(8,128)S(1)}, u32[]{:S(2)}, u32[]{:S(2)}) collective-permute-start(f32[2,128,128]{2,1,0:T(8,128)S(1)} %copy-done.32), channel_id=1, source_target_pairs={{0,24},{8,0},{16,8},{24,16},{1,25},{9,1},{17,9},{25,17},{2,26},{10... | collective-permute-start | bytes 393224 | tf_op jit(solution)/shard_map/ppermute | solution.py:372
  160.3 3.9 %finish_rank.7 = (f32[2,128,128]{2,1,0:T(8,128)}, f32[2,128,128]{2,1,0:T(8,128)}, f32[2,128,128]{2,1,0:T(8,128)}, f32[2,128,128]{2,1,0:T(8,128)}) custom-call(s32[2]{0:T(128)} %pad_add_fusion.1.refs_6_.meta_ref, s32[8,32]{1,0:T(8,128)} %select_reduce_fusion.words_ref, s32[8,32]{1,0:T(8,128)} %select_reduce_fusion.4.refs_5_.fillers_ref, ...), custom_call_target="tpu_custom_call" | custom-call | flops 201326592 | tf_op jit(solution)/shard_map/finish_rank/pallas_call | solution.py:322
  164.3 2.1 %collective-permute-start.30 = (f32[2,128,128]{2,1,0:T(8,128)S(1)}, f32[2,128,128]{2,1,0:T(8,128)S(1)}, u32[]{:S(2)}, u32[]{:S(2)}) collective-permute-start(f32[2,128,128]{2,1,0:T(8,128)S(1)} %copy-done.33), channel_id=1, source_target_pairs={{0,16},{8,24},{16,0},{24,8},{1,17},{9,25},{17,1},{25,9},{2,18},{10... | collective-permute-start | bytes 393224 | tf_op jit(solution)/shard_map/ppermute | solution.py:372
  166.3 2.2 %collective-permute-start.31 = (f32[2,128,128]{2,1,0:T(8,128)S(1)}, f32[2,128,128]{2,1,0:T(8,128)S(1)}, u32[]{:S(2)}, u32[]{:S(2)}) collective-permute-start(f32[2,128,128]{2,1,0:T(8,128)S(1)} %copy-done.31), channel_id=1, source_target_pairs={{0,24},{8,0},{16,8},{24,16},{1,25},{9,1},{17,9},{25,17},{2,26},{10... | collective-permute-start | bytes 393224 | tf_op jit(solution)/shard_map/ppermute | solution.py:372
  169.6 7.5 %collective-permute-start.35 = (f32[2,128,128]{2,1,0:T(8,128)}, f32[2,128,128]{2,1,0:T(8,128)S(1)}, u32[]{:S(2)}, u32[]{:S(2)}) collective-permute-start(f32[2,128,128]{2,1,0:T(8,128)} %get-tuple-element.63), channel_id=1, source_target_pairs={{0,16},{8,24},{16,0},{24,8},{1,17},{9,25},{17,1},{25,9},{2,18},{10... | collective-permute-start | bytes 393224 | tf_op jit(solution)/shard_map/ppermute | solution.py:372
  177.0 3.9 %collective-permute-start.36 = (f32[2,128,128]{2,1,0:T(8,128)}, f32[2,128,128]{2,1,0:T(8,128)S(1)}, u32[]{:S(2)}, u32[]{:S(2)}) collective-permute-start(f32[2,128,128]{2,1,0:T(8,128)} %get-tuple-element.64), channel_id=1, source_target_pairs={{0,24},{8,0},{16,8},{24,16},{1,25},{9,1},{17,9},{25,17},{2,26},{10... | collective-permute-start | bytes 393224 | tf_op jit(solution)/shard_map/ppermute | solution.py:372
  180.9 5.1 %collective-permute-done.30.refs_10_ = f32[2,128,128]{2,1,0:T(8,128)S(1)} collective-permute-done((f32[2,128,128]{2,1,0:T(8,128)S(1)}, f32[2,128,128]{2,1,0:T(8,128)S(1)}, u32[]{:S(2)}, u32[]{:S(2)}) %collective-permute-start.30) | collective-permute-done | bytes 131104 | tf_op jit(solution)/shard_map/ppermute | solution.py:372
  186.0 5.6 %collective-permute-done.35.refs_14_ = f32[2,128,128]{2,1,0:T(8,128)S(1)} collective-permute-done((f32[2,128,128]{2,1,0:T(8,128)}, f32[2,128,128]{2,1,0:T(8,128)S(1)}, u32[]{:S(2)}, u32[]{:S(2)}) %collective-permute-start.35) | collective-permute-done | bytes 131104 | tf_op jit(solution)/shard_map/ppermute | solution.py:372
  192.3 2.5 %place_sums.1 = f32[8,128,128]{2,1,0:T(8,128)} custom-call(s32[2]{0:T(128)} %pad_add_fusion.1.refs_6_.meta_ref, s32[8,32]{1,0:T(8,128)} %select_reduce_fusion.4.refs_5_.fillers_ref, f32[2,128,128]{2,1,0:T(8,128)} %get-tuple-element.45.refs_8_.refs_0_, f32[2,128,128]{2,1,0:T(8,128)} %copy-done.16, f32[2,128,128]{2,1,0:T(8,128)} %collective-permute-done.16.refs_2_, ...), custom_call_target="tpu_custom_call" | custom-call | flops 100663296 | tf_op jit(solution)/shard_map/place_sums/pallas_call | solution.py:355
  (184 shorter events, 37.8 us)
Async XLA Ops:
  0.0 78.0 %collective-permute-start.4 = (bf16[1536,1024]{1,0:T(8,128)(2,1)}, bf16[1536,1024]{1,0:T(8,128)(2,1)}, u32[]{:S(2)}, u32[]{:S(2)}) collective-permute-start(bf16[1536,1024]{1,0:T(8,128)(2,1)} %shard_ref.5), channel_id=1, source_target_pairs={{0,1},{1,0},{2,3},{3,2},{4,5},{5,4},{6,7},{7,6},{8,9},{9,8},{10,11... | collective-permute-start | bytes 9437192 | tf_op jit(solution)/shard_map/ppermute | solution.py:367
  14.3 21.2 %collective-permute-start.1 = (bf16[3,1024,128]{2,1,0:T(8,128)(2,1)}, bf16[3,1024,128]{2,1,0:T(8,128)(2,1)S(1)}, u32[]{:S(2)}, u32[]{:S(2)}) collective-permute-start(bf16[3,1024,128]{2,1,0:T(8,128)(2,1)} %get-tuple-element.35.refs_0_), channel_id=1, source_target_pairs={{0,2},{1,3},{2,0},{3,1},{4,6},{5,7},{6,4},{7,5},{8,10},{9,11},{10,... | collective-permute-start | bytes 2359304 | tf_op jit(solution)/shard_map/ppermute | solution.py:367
  16.9 20.7 %collective-permute-start.3 = (bf16[3,1024,128]{2,1,0:T(8,128)(2,1)}, bf16[3,1024,128]{2,1,0:T(8,128)(2,1)}, u32[]{:S(2)}, u32[]{:S(2)}) collective-permute-start(bf16[3,1024,128]{2,1,0:T(8,128)(2,1)} %get-tuple-element.36.refs_1_), channel_id=1, source_target_pairs={{0,4},{1,5},{2,6},{3,7},{4,0},{5,1},{6,2},{7,3},{8,12},{9,13},{10,... | collective-permute-start | bytes 2359304 | tf_op jit(solution)/shard_map/ppermute | solution.py:367
  21.4 31.0 %collective-permute-start.11 = (bf16[3,1024,128]{2,1,0:T(8,128)(2,1)}, bf16[3,1024,128]{2,1,0:T(8,128)(2,1)}, u32[]{:S(2)}, u32[]{:S(2)}) collective-permute-start(bf16[3,1024,128]{2,1,0:T(8,128)(2,1)} %get-tuple-element.37.refs_3_), channel_id=1, source_target_pairs={{0,2},{1,3},{2,0},{3,1},{4,6},{5,7},{6,4},{7,5},{8,10},{9,11},{10,... | collective-permute-start | bytes 2359304 | tf_op jit(solution)/shard_map/ppermute | solution.py:367
  24.3 35.7 %collective-permute-start.2 = (bf16[512,1024]{1,0:T(8,128)(2,1)}, bf16[512,1024]{1,0:T(8,128)(2,1)S(1)}, u32[]{:S(2)}, u32[]{:S(2)}) collective-permute-start(bf16[512,1024]{1,0:T(8,128)(2,1)} %slice.3), channel_id=1, source_target_pairs={{0,4},{1,5},{2,6},{3,7},{4,0},{5,1},{6,2},{7,3},{8,12},{9,13},{10,... | collective-permute-start | bytes 3145736 | tf_op jit(solution)/shard_map/ppermute | solution.py:367
  35.5 39.1 %collective-permute-start = (bf16[512,1024]{1,0:T(8,128)(2,1)}, bf16[512,1024]{1,0:T(8,128)(2,1)S(1)}, u32[]{:S(2)}, u32[]{:S(2)}) collective-permute-start(bf16[512,1024]{1,0:T(8,128)(2,1)} %slice.3), channel_id=1, source_target_pairs={{0,2},{1,3},{2,0},{3,1},{4,6},{5,7},{6,4},{7,5},{8,10},{9,11},{10,... | collective-permute-start | bytes 3145736 | tf_op jit(solution)/shard_map/ppermute | solution.py:367
  37.6 38.6 %collective-permute-start.12 = (bf16[3,1024,128]{2,1,0:T(8,128)(2,1)}, bf16[3,1024,128]{2,1,0:T(8,128)(2,1)}, u32[]{:S(2)}, u32[]{:S(2)}) collective-permute-start(bf16[3,1024,128]{2,1,0:T(8,128)(2,1)} %get-tuple-element.38.refs_4_), channel_id=1, source_target_pairs={{0,4},{1,5},{2,6},{3,7},{4,0},{5,1},{6,2},{7,3},{8,12},{9,13},{10,... | collective-permute-start | bytes 2359304 | tf_op jit(solution)/shard_map/ppermute | solution.py:367
  52.5 23.7 %collective-permute-start.8 = (bf16[3,1024,128]{2,1,0:T(8,128)(2,1)S(1)}, bf16[3,1024,128]{2,1,0:T(8,128)(2,1)}, u32[]{:S(2)}, u32[]{:S(2)}) collective-permute-start(bf16[3,1024,128]{2,1,0:T(8,128)(2,1)S(1)} %collective-permute-done.1.refs_1_), channel_id=1, source_target_pairs={{0,1},{1,0},{2,3},{3,2},{4,5},{5,4},{6,7},{7,6},{8,9},{9,8},{10,11... | collective-permute-start | bytes 2359304 | tf_op jit(solution)/shard_map/ppermute | solution.py:367
  60.0 32.8 %collective-permute-start.9 = (bf16[512,1024]{1,0:T(8,128)(2,1)S(1)}, bf16[512,1024]{1,0:T(8,128)(2,1)}, u32[]{:S(2)}, u32[]{:S(2)}) collective-permute-start(bf16[512,1024]{1,0:T(8,128)(2,1)S(1)} %collective-permute-done.2.refs_2_.refs_3_.refs_4_), channel_id=1, source_target_pairs={{0,1},{1,0},{2,3},{3,2},{4,5},{5,4},{6,7},{7,6},{8,9},{9,8},{10,11... | collective-permute-start | bytes 3145736 | tf_op jit(solution)/shard_map/ppermute | solution.py:367
  74.6 19.5 %collective-permute-start.7 = (bf16[512,1024]{1,0:T(8,128)(2,1)S(1)}, bf16[512,1024]{1,0:T(8,128)(2,1)}, u32[]{:S(2)}, u32[]{:S(2)}) collective-permute-start(bf16[512,1024]{1,0:T(8,128)(2,1)S(1)} %collective-permute-done.refs_0_), channel_id=1, source_target_pairs={{0,1},{1,0},{2,3},{3,2},{4,5},{5,4},{6,7},{7,6},{8,9},{9,8},{10,11... | collective-permute-start | bytes 3145736 | tf_op jit(solution)/shard_map/ppermute | solution.py:367
  76.2 14.3 %collective-permute-start.10 = (bf16[3,1024,128]{2,1,0:T(8,128)(2,1)}, bf16[3,1024,128]{2,1,0:T(8,128)(2,1)}, u32[]{:S(2)}, u32[]{:S(2)}) collective-permute-start(bf16[3,1024,128]{2,1,0:T(8,128)(2,1)} %collective-permute-done.3.refs_3_.refs_4_.refs_5_), channel_id=1, source_target_pairs={{0,1},{1,0},{2,3},{3,2},{4,5},{5,4},{6,7},{7,6},{8,9},{9,8},{10,11... | collective-permute-start | bytes 2359304 | tf_op jit(solution)/shard_map/ppermute | solution.py:367
  76.2 15.1 %collective-permute-start.13 = (bf16[3,1024,128]{2,1,0:T(8,128)(2,1)}, bf16[3,1024,128]{2,1,0:T(8,128)(2,1)}, u32[]{:S(2)}, u32[]{:S(2)}) collective-permute-start(bf16[3,1024,128]{2,1,0:T(8,128)(2,1)} %collective-permute-done.11.refs_2_), channel_id=1, source_target_pairs={{0,1},{1,0},{2,3},{3,2},{4,5},{5,4},{6,7},{7,6},{8,9},{9,8},{10,11... | collective-permute-start | bytes 2359304 | tf_op jit(solution)/shard_map/ppermute | solution.py:367
  78.0 23.0 %collective-permute-start.14 = (bf16[3,1024,128]{2,1,0:T(8,128)(2,1)}, bf16[3,1024,128]{2,1,0:T(8,128)(2,1)}, u32[]{:S(2)}, u32[]{:S(2)}) collective-permute-start(bf16[3,1024,128]{2,1,0:T(8,128)(2,1)} %collective-permute-done.12.refs_5_.refs_6_), channel_id=1, source_target_pairs={{0,1},{1,0},{2,3},{3,2},{4,5},{5,4},{6,7},{7,6},{8,9},{9,8},{10,11... | collective-permute-start | bytes 2359304 | tf_op jit(solution)/shard_map/ppermute | solution.py:367
  90.5 28.8 %collective-permute-start.20 = (bf16[2,1024,128]{2,1,0:T(8,128)(2,1)}, bf16[2,1024,128]{2,1,0:T(8,128)(2,1)S(1)}, u32[]{:S(2)}, u32[]{:S(2)}) collective-permute-start(bf16[2,1024,128]{2,1,0:T(8,128)(2,1)} %get-tuple-element.41.refs_9_), channel_id=1, source_target_pairs={{0,2},{1,3},{2,0},{3,1},{4,6},{5,7},{6,4},{7,5},{8,10},{9,11},{10,... | collective-permute-start | bytes 1572872 | tf_op jit(solution)/shard_map/ppermute | solution.py:367
  91.3 28.1 %collective-permute-start.21 = (bf16[2,1024,128]{2,1,0:T(8,128)(2,1)}, bf16[2,1024,128]{2,1,0:T(8,128)(2,1)S(1)}, u32[]{:S(2)}, u32[]{:S(2)}) collective-permute-start(bf16[2,1024,128]{2,1,0:T(8,128)(2,1)} %get-tuple-element.42.refs_10_), channel_id=1, source_target_pairs={{0,4},{1,5},{2,6},{3,7},{4,0},{5,1},{6,2},{7,3},{8,12},{9,13},{10,... | collective-permute-start | bytes 1572872 | tf_op jit(solution)/shard_map/ppermute | solution.py:367
  92.8 21.2 %collective-permute-start.5 = (bf16[1,1536,128]{2,1,0:T(8,128)(2,1)S(1)}, bf16[1,1536,128]{2,1,0:T(8,128)(2,1)S(1)}, u32[]{:S(2)}, u32[]{:S(2)}) collective-permute-start(bf16[1,1536,128]{2,1,0:T(8,128)(2,1)S(1)} %copy-done.15), channel_id=1, source_target_pairs={{0,2},{1,3},{2,0},{3,1},{4,6},{5,7},{6,4},{7,5},{8,10},{9,11},{10,... | collective-permute-start | bytes 1179656 | tf_op jit(solution)/shard_map/ppermute | solution.py:367
  94.1 20.2 %collective-permute-start.6 = (bf16[1,1536,128]{2,1,0:T(8,128)(2,1)}, bf16[1,1536,128]{2,1,0:T(8,128)(2,1)S(1)}, u32[]{:S(2)}, u32[]{:S(2)}) collective-permute-start(bf16[1,1536,128]{2,1,0:T(8,128)(2,1)} %get-tuple-element.40.refs_1_), channel_id=1, source_target_pairs={{0,5},{1,4},{2,7},{3,6},{4,1},{5,0},{6,3},{7,2},{8,13},{9,12},{10,... | collective-permute-start | bytes 1179656 | tf_op jit(solution)/shard_map/ppermute | solution.py:367
  101.0 23.9 %collective-permute-start.18 = (bf16[1,1536,128]{2,1,0:T(8,128)(2,1)}, bf16[1,1536,128]{2,1,0:T(8,128)(2,1)S(1)}, u32[]{:S(2)}, u32[]{:S(2)}) collective-permute-start(bf16[1,1536,128]{2,1,0:T(8,128)(2,1)} %get-tuple-element.43.refs_13_), channel_id=1, source_target_pairs={{0,2},{1,3},{2,0},{3,1},{4,6},{5,7},{6,4},{7,5},{8,10},{9,11},{10,... | collective-permute-start | bytes 1179656 | tf_op jit(solution)/shard_map/ppermute | solution.py:367
  124.9 12.7 %collective-permute-start.23 = (bf16[2,1024,128]{2,1,0:T(8,128)(2,1)}, bf16[2,1024,128]{2,1,0:T(8,128)(2,1)S(1)}, u32[]{:S(2)}, u32[]{:S(2)}) collective-permute-start(bf16[2,1024,128]{2,1,0:T(8,128)(2,1)} %copy-done.4), channel_id=1, source_target_pairs={{0,1},{1,0},{2,3},{3,2},{4,5},{5,4},{6,7},{7,6},{8,9},{9,8},{10,11... | collective-permute-start | bytes 1572872 | tf_op jit(solution)/shard_map/ppermute | solution.py:367
  124.9 25.2 %collective-permute-start.28 = (bf16[1,1536,128]{2,1,0:T(8,128)(2,1)}, bf16[1,1536,128]{2,1,0:T(8,128)(2,1)S(1)}, u32[]{:S(2)}, u32[]{:S(2)}) collective-permute-start(bf16[1,1536,128]{2,1,0:T(8,128)(2,1)} %get-tuple-element.50.refs_18_), channel_id=1, source_target_pairs={{0,5},{1,4},{2,7},{3,6},{4,1},{5,0},{6,3},{7,2},{8,13},{9,12},{10,... | collective-permute-start | bytes 1179656 | tf_op jit(solution)/shard_map/ppermute | solution.py:367
  126.0 31.1 %collective-permute-start.32 = (bf16[1,1536,128]{2,1,0:T(8,128)(2,1)}, bf16[1,1536,128]{2,1,0:T(8,128)(2,1)S(1)}, u32[]{:S(2)}, u32[]{:S(2)}) collective-permute-start(bf16[1,1536,128]{2,1,0:T(8,128)(2,1)} %get-tuple-element.51.refs_19_), channel_id=1, source_target_pairs={{0,2},{1,3},{2,0},{3,1},{4,6},{5,7},{6,4},{7,5},{8,10},{9,11},{10,... | collective-permute-start | bytes 1179656 | tf_op jit(solution)/shard_map/ppermute | solution.py:367
  135.7 23.8 %collective-permute-start.33 = (bf16[1,1536,128]{2,1,0:T(8,128)(2,1)}, bf16[1,1536,128]{2,1,0:T(8,128)(2,1)S(1)}, u32[]{:S(2)}, u32[]{:S(2)}) collective-permute-start(bf16[1,1536,128]{2,1,0:T(8,128)(2,1)} %get-tuple-element.52.refs_20_), channel_id=1, source_target_pairs={{0,5},{1,4},{2,7},{3,6},{4,1},{5,0},{6,3},{7,2},{8,13},{9,12},{10,... | collective-permute-start | bytes 1179656 | tf_op jit(solution)/shard_map/ppermute | solution.py:367
  135.7 19.8 %collective-permute-start.15 = (f32[2,128,128]{2,1,0:T(8,128)}, f32[2,128,128]{2,1,0:T(8,128)S(1)}, u32[]{:S(2)}, u32[]{:S(2)}) collective-permute-start(f32[2,128,128]{2,1,0:T(8,128)} %get-tuple-element.46), channel_id=1, source_target_pairs={{0,8},{8,16},{16,24},{24,0},{1,9},{9,17},{17,25},{25,1},{2,10},{10... | collective-permute-start | bytes 393224 | tf_op jit(solution)/shard_map/ppermute | solution.py:372
  137.6 18.7 %collective-permute-start.16 = (f32[2,128,128]{2,1,0:T(8,128)}, f32[2,128,128]{2,1,0:T(8,128)}, u32[]{:S(2)}, u32[]{:S(2)}) collective-permute-start(f32[2,128,128]{2,1,0:T(8,128)} %get-tuple-element.47), channel_id=1, source_target_pairs={{0,16},{8,24},{16,0},{24,8},{1,17},{9,25},{17,1},{25,9},{2,18},{10... | collective-permute-start | bytes 393224 | tf_op jit(solution)/shard_map/ppermute | solution.py:372
  150.1 14.1 %collective-permute-start.17 = (f32[2,128,128]{2,1,0:T(8,128)S(1)}, f32[2,128,128]{2,1,0:T(8,128)S(1)}, u32[]{:S(2)}, u32[]{:S(2)}) collective-permute-start(f32[2,128,128]{2,1,0:T(8,128)S(1)} %copy-done.30), channel_id=1, source_target_pairs={{0,24},{8,0},{16,8},{24,16},{1,25},{9,1},{17,9},{25,17},{2,26},{10... | collective-permute-start | bytes 393224 | tf_op jit(solution)/shard_map/ppermute | solution.py:372
  156.3 13.2 %collective-permute-start.25 = (f32[2,128,128]{2,1,0:T(8,128)S(1)}, f32[2,128,128]{2,1,0:T(8,128)S(1)}, u32[]{:S(2)}, u32[]{:S(2)}) collective-permute-start(f32[2,128,128]{2,1,0:T(8,128)S(1)} %copy-done.34), channel_id=1, source_target_pairs={{0,16},{8,24},{16,0},{24,8},{1,17},{9,25},{17,1},{25,9},{2,18},{10... | collective-permute-start | bytes 393224 | tf_op jit(solution)/shard_map/ppermute | solution.py:372
  159.5 17.5 %collective-permute-start.29 = (f32[2,128,128]{2,1,0:T(8,128)}, f32[2,128,128]{2,1,0:T(8,128)S(1)}, u32[]{:S(2)}, u32[]{:S(2)}) collective-permute-start(f32[2,128,128]{2,1,0:T(8,128)} %get-tuple-element.58), channel_id=1, source_target_pairs={{0,8},{8,16},{16,24},{24,0},{1,9},{9,17},{17,25},{25,1},{2,10},{10... | collective-permute-start | bytes 393224 | tf_op jit(solution)/shard_map/ppermute | solution.py:372
  164.3 21.7 %collective-permute-start.30 = (f32[2,128,128]{2,1,0:T(8,128)S(1)}, f32[2,128,128]{2,1,0:T(8,128)S(1)}, u32[]{:S(2)}, u32[]{:S(2)}) collective-permute-start(f32[2,128,128]{2,1,0:T(8,128)S(1)} %copy-done.33), channel_id=1, source_target_pairs={{0,16},{8,24},{16,0},{24,8},{1,17},{9,25},{17,1},{25,9},{2,18},{10... | collective-permute-start | bytes 393224 | tf_op jit(solution)/shard_map/ppermute | solution.py:372
  166.3 19.6 %collective-permute-start.31 = (f32[2,128,128]{2,1,0:T(8,128)S(1)}, f32[2,128,128]{2,1,0:T(8,128)S(1)}, u32[]{:S(2)}, u32[]{:S(2)}) collective-permute-start(f32[2,128,128]{2,1,0:T(8,128)S(1)} %copy-done.31), channel_id=1, source_target_pairs={{0,24},{8,0},{16,8},{24,16},{1,25},{9,1},{17,9},{25,17},{2,26},{10... | collective-permute-start | bytes 393224 | tf_op jit(solution)/shard_map/ppermute | solution.py:372
  169.5 16.4 %collective-permute-start.34 = (f32[2,128,128]{2,1,0:T(8,128)}, f32[2,128,128]{2,1,0:T(8,128)S(1)}, u32[]{:S(2)}, u32[]{:S(2)}) collective-permute-start(f32[2,128,128]{2,1,0:T(8,128)} %get-tuple-element.62), channel_id=1, source_target_pairs={{0,8},{8,16},{16,24},{24,0},{1,9},{9,17},{17,25},{25,1},{2,10},{10... | collective-permute-start | bytes 393224 | tf_op jit(solution)/shard_map/ppermute | solution.py:372
  169.6 22.0 %collective-permute-start.35 = (f32[2,128,128]{2,1,0:T(8,128)}, f32[2,128,128]{2,1,0:T(8,128)S(1)}, u32[]{:S(2)}, u32[]{:S(2)}) collective-permute-start(f32[2,128,128]{2,1,0:T(8,128)} %get-tuple-element.63), channel_id=1, source_target_pairs={{0,16},{8,24},{16,0},{24,8},{1,17},{9,25},{17,1},{25,9},{2,18},{10... | collective-permute-start | bytes 393224 | tf_op jit(solution)/shard_map/ppermute | solution.py:372
  177.0 14.6 %collective-permute-start.36 = (f32[2,128,128]{2,1,0:T(8,128)}, f32[2,128,128]{2,1,0:T(8,128)S(1)}, u32[]{:S(2)}, u32[]{:S(2)}) collective-permute-start(f32[2,128,128]{2,1,0:T(8,128)} %get-tuple-element.64), channel_id=1, source_target_pairs={{0,24},{8,0},{16,8},{24,16},{1,25},{9,1},{17,9},{25,17},{2,26},{10... | collective-permute-start | bytes 393224 | tf_op jit(solution)/shard_map/ppermute | solution.py:372
  (41 other events, 592.9 us)
